TPU v7x, 64 devices: a 2x2x8 block of a 4x4x8 slice. The times are simulated.
64 devices in a mesh: dp: 4 (over x, y), tp: 16 (over z, core).
Axes of the slice: x: 2, y: 2, z: 8, core: 2. Of those that a mesh axis runs over, the one named last changes fastest.
The devices are a block of a 4x4x8 slice.
Arguments:
- x_in: bfloat16 [512, 4096], P('dp'), parts along dimension 0
- lengths: int32 [512], P('dp'), parts along dimension 0
- norm_gain: bfloat16 [2, 4096], replicated
- w_q: bfloat16 [2, 4096, 4096], P(None, None, 'tp')
- w_k: bfloat16 [2, 4096, 4096], P(None, None, 'tp')
- w_v: bfloat16 [2, 4096, 4096], P(None, None, 'tp')
- w_o: bfloat16 [2, 4096, 4096], P(None, 'tp')
- w_gate: bfloat16 [2, 4096, 11008], P(None, None, 'tp')
- w_up: bfloat16 [2, 4096, 11008], P(None, None, 'tp')
- w_down: bfloat16 [2, 11008, 4096], P(None, 'tp')
- k_cache: bfloat16 [2, 512, 32, 32, 128], P(None, 'dp', None, 'tp'), parts along dimension 1
- v_cache: bfloat16 [2, 512, 32, 32, 128], P(None, 'dp', None, 'tp'), parts along dimension 1
Outputs:
- output: bfloat16 [512, 4096], P('dp'), parts along dimension 0
There are 4 independent parts. A program takes and returns all parts, laid end to end along the dimension named above; an argument that names none is the same for every part.
All inputs are finite; a program needn't handle non-finite values.
Results may differ from a plain program's by a relative error of at most 0.0174662.
Values are sent between devices in bfloat16 or wider.
A program may use at most 768 MiB of HBM per device.

v0:
```python
import jax
import jax.numpy as jnp
from jax import lax
from jax.sharding import PartitionSpec as P

NORM_EPS = 1e-5
ROPE_BASE = 500000.0


def rms_norm(x_res, gain_row):
    x_f32 = x_res.astype(jnp.float32)
    inv_rms = lax.rsqrt(jnp.mean(x_f32 * x_f32, axis=-1, keepdims=True) + NORM_EPS)
    return (x_f32 * inv_rms * gain_row.astype(jnp.float32)).astype(jnp.bfloat16)


def rope_rotate(head_vecs, positions):
    head_dim = head_vecs.shape[-1]
    half_dim = head_dim // 2
    inv_freq = 1.0 / (ROPE_BASE ** (jnp.arange(0, head_dim, 2).astype(jnp.float32) / head_dim))
    angles = positions.astype(jnp.float32)[:, None] * inv_freq[None, :]
    cos_ang = jnp.cos(angles)[:, None, :]
    sin_ang = jnp.sin(angles)[:, None, :]
    vec_f32 = head_vecs.astype(jnp.float32)
    rot_first = vec_f32[..., :half_dim]
    rot_second = vec_f32[..., half_dim:]
    return jnp.concatenate([rot_first * cos_ang - rot_second * sin_ang, rot_second * cos_ang + rot_first * sin_ang], axis=-1).astype(jnp.bfloat16)


def decode_attention(q_rot, k_rot, v_new, k_layer, v_layer, lengths):
    attn_scale = q_rot.shape[-1] ** -0.5
    seq_len = k_layer.shape[1]
    cache_logits = jnp.einsum('bkgd,bskd->bkgs', q_rot, k_layer, preferred_element_type=jnp.float32) * attn_scale
    valid_mask = jnp.arange(seq_len)[None, :] < lengths[:, None]
    cache_logits = jnp.where(valid_mask[:, None, None, :], cache_logits, -jnp.inf)
    self_logit = jnp.einsum('clhe,cle->clh', q_rot, k_rot, preferred_element_type=jnp.float32) * attn_scale
    row_peak = jnp.maximum(jnp.max(cache_logits, axis=-1), self_logit)
    cache_w = jnp.exp(cache_logits - row_peak[..., None])
    self_w = jnp.exp(self_logit - row_peak)
    prob_denom = jnp.sum(cache_w, axis=-1) + self_w
    cache_p = (cache_w / prob_denom[..., None]).astype(jnp.bfloat16)
    self_p = (self_w / prob_denom).astype(jnp.bfloat16)
    cache_part = jnp.einsum('bkgs,bskd->bkgd', cache_p, v_layer, preferred_element_type=jnp.float32)
    self_part = self_p.astype(jnp.float32)[..., None] * v_new.astype(jnp.float32)[:, :, None, :]
    return (cache_part + self_part).astype(jnp.bfloat16)


def layer_update(x_res, lengths, gain_row, wq_layer, wk_layer, wv_layer, wo_layer, wg_layer, wu_layer, wd_layer, k_layer, v_layer):
    tok_rows = x_res.shape[0]
    head_dim = k_layer.shape[-1]
    kv_local = k_layer.shape[-2]
    normed = rms_norm(x_res, gain_row)
    q_proj = jnp.dot(normed, wq_layer, preferred_element_type=jnp.float32).astype(jnp.bfloat16).reshape(tok_rows, -1, head_dim)
    k_proj = jnp.dot(normed, wk_layer, preferred_element_type=jnp.float32).astype(jnp.bfloat16).reshape(tok_rows, kv_local, head_dim)
    v_new = jnp.dot(normed, wv_layer, preferred_element_type=jnp.float32).astype(jnp.bfloat16).reshape(tok_rows, kv_local, head_dim)
    q_rot = rope_rotate(q_proj, lengths).reshape(tok_rows, kv_local, -1, head_dim)
    k_rot = rope_rotate(k_proj, lengths)
    attn_flat = decode_attention(q_rot, k_rot, v_new, k_layer, v_layer, lengths).reshape(tok_rows, -1)
    gate_act = jnp.dot(normed, wg_layer, preferred_element_type=jnp.float32).astype(jnp.bfloat16)
    up_act = jnp.dot(normed, wu_layer, preferred_element_type=jnp.float32).astype(jnp.bfloat16)
    mlp_hidden = (jax.nn.silu(gate_act.astype(jnp.float32)) * up_act.astype(jnp.float32)).astype(jnp.bfloat16)
    return jnp.dot(attn_flat, wo_layer, preferred_element_type=jnp.float32) + jnp.dot(mlp_hidden, wd_layer, preferred_element_type=jnp.float32)


def solution(mesh):
    tp_size = mesh.shape['tp']
    arg_specs = (P('dp', None), P('dp'), P(), P(None, None, 'tp'), P(None, None, 'tp'), P(None, None, 'tp'), P(None, 'tp', None), P(None, None, 'tp'), P(None, None, 'tp'), P(None, 'tp', None), P(None, 'dp', None, 'tp', None), P(None, 'dp', None, 'tp', None))

    def per_device(x_in, lengths, norm_gain, w_q, w_k, w_v, w_o, w_gate, w_up, w_down, k_cache, v_cache):
        tok_rows, model_width = x_in.shape
        col_width = model_width // tp_size
        col_start = lax.axis_index('tp') * col_width
        x_res = x_in
        for layer_idx in range(norm_gain.shape[0]):
            update = layer_update(x_res, lengths, norm_gain[layer_idx], w_q[layer_idx], w_k[layer_idx], w_v[layer_idx], w_o[layer_idx], w_gate[layer_idx], w_up[layer_idx], w_down[layer_idx], k_cache[layer_idx], v_cache[layer_idx])
            partial_sum = update.astype(jnp.bfloat16)
            received = lax.all_to_all(partial_sum, 'tp', 1, 0, tiled=True)
            reduced = jnp.sum(received.reshape(tp_size, tok_rows, col_width).astype(jnp.float32), axis=0)
            own_cols = lax.dynamic_slice_in_dim(x_res, col_start, col_width, axis=1)
            new_cols = (own_cols.astype(jnp.float32) + reduced).astype(jnp.bfloat16)
            x_res = lax.all_gather(new_cols, 'tp', axis=1, tiled=True)
        return x_res

    return jax.shard_map(per_device, mesh=mesh, in_specs=arg_specs, out_specs=P('dp', None), check_vma=False)
```

profile of v0, /device:TPU:21, one launch (start us, length us, event | category | flops | bytes accessed | tf_op | source)
XLA Modules:
  0.0 239.7 jit_solution(14580099956582089284)
XLA Ops:
  6.6 0.7 convert_element_type.190
  7.2 0.7 iota_compare_fusion
  7.9 1.4 slice_convert_fusion
  9.3 1.5 fusion.20
  10.8 2.5 %fusion.125 = f32[128,256]{1,0:T(8,128)S(1)} fusion(bf16[2,4096,256]{2,1,0:T(8,128)(2,1)} %param.15, bf16[128,4096]{1,0:T(8,128)(2,1)} %param.12, f32[4096]{0:T(1024)S(1)} %bitcast.170, f32[128]{0:T(128)S(1)} %add_rsqrt_fusion.1), kind=kOutput, calls=%fused_computation.91 | convolution fusion | flops 270598144 | bytes 3293696 | tf_op jit(solution)/shard_map/dot_general | solution.py:52
  13.3 0.1 reshape.233
  13.4 2.1 fusion.122
  15.5 0.1 reshape.234
  15.6 0.3 multiply_cosine_fusion
  15.9 0.4 subtract_convert_fusion.2
  16.3 0.2 fusion.167
  16.5 0.5 fusion.145
  17.1 0.1 copy.25
  17.1 6.0 %slice_bitcast_fusion.1 = (bf16[128,32,2,128]{3,2,1,0:T(2,128)(2,1)}, bf16[128,32,2,128]{3,2,1,0:T(2,128)(2,1)S(1)}) fusion(bf16[2,128,32,2,128]{4,3,2,1,0:T(2,128)(2,1)} %param.22), kind=kLoop, calls=%fused_computation.59 | loop fusion | bytes 8388608 | tf_op jit(solution)/shard_map/squeeze | solution.py:74
  23.1 1.2 fusion.46
  24.2 0.1 copy.21
  24.5 0.8 copy.26
  25.2 7.1 %slice_bitcast_fusion = (bf16[128,32,2,128]{3,2,1,0:T(2,128)(2,1)S(1)}, bf16[128,32,2,128]{3,2,1,0:T(2,128)(2,1)}) fusion(bf16[2,128,32,2,128]{4,3,2,1,0:T(2,128)(2,1)} %param.23), kind=kLoop, calls=%fused_computation.57 | loop fusion | bytes 8388608 | tf_op jit(solution)/shard_map/squeeze | solution.py:74
  32.3 0.1 copy.15
  32.5 2.7 %fusion.119 = f32[128,256]{1,0:T(8,128)} fusion(bf16[2,4096,256]{2,1,0:T(8,128)(2,1)} %param.17, bf16[128,4096]{1,0:T(8,128)(2,1)S(1)} %copy-done.1, f32[4096]{0:T(1024)S(1)} %bitcast.173, f32[128]{0:T(128)S(1)} %add_rsqrt_fusion.1), kind=kOutput, calls=%fused_computation.89 | convolution fusion | flops 270598144 | bytes 3293696 | tf_op jit(solution)/shard_map/dot_general | solution.py:54
  35.2 1.0 reshape.235
  36.2 5.2 %fusion.59 = f32[128,688]{0,1:T(8,128)} fusion(bf16[2,4096,688]{1,2,0:T(8,128)(2,1)} %param.19, bf16[128,4096]{1,0:T(8,128)(2,1)S(1)} %copy-done.1, f32[4096]{0:T(1024)S(1)} %bitcast.174, f32[128]{0:T(128)S(1)} %add_rsqrt_fusion.1), kind=kOutput, calls=%fused_computation.69 | convolution fusion | flops 723693568 | bytes 7053824 | tf_op jit(solution)/shard_map/dot_general | solution.py:58
  41.4 0.6 fusion.44
  42.0 0.2 add_convert_fusion.5
  42.2 9.9 %fusion.6 = f32[128,4096]{1,0:T(8,128)} fusion(bf16[2,688,4096]{2,1,0:T(8,128)(2,1)} %param.21, bf16[2,4096,688]{1,2,0:T(8,128)(2,1)} %param.20, f32[128,688]{0,1:T(8,128)} %fusion.59, bf16[128,4096]{1,0:T(8,128)(2,1)S(1)} %copy-done.1, f32[4096]{0:T(1024)} %bitcast.172, f32[128]{0:T(128)S(1)} %add_rsqrt_fusion.1), kind=kOutput, calls=%fused_computation.6 | convolution fusion | flops 1445642240 | bytes 14787072 | tf_op jit(solution)/shard_map/dot_general | solution.py:61
  52.1 2.7 %fusion.18 = bf16[128,4096]{1,0:T(8,128)(2,1)S(1)} fusion(f32[128,4096]{1,0:T(8,128)} %fusion.6, bf16[2,256,4096]{2,1,0:T(8,128)(2,1)} %param.18, bf16[16,8,2,128]{3,2,1,0:T(2,128)(2,1)S(1)} %bitcast.162), kind=kOutput, calls=%fused_computation.20 | convolution fusion | flops 269484032 | bytes 5308416 | tf_op jit(solution)/shard_map/dot_general | solution.py:61
  54.8 1.1 copy.68
  55.9 10.9 %all-to-all-start = ((bf16[128,16,256]{2,0,1:T(8,128)(2,1)}), bf16[128,16,256]{2,0,1:T(8,128)(2,1)S(1)}, u32[]{:S(2)}, u32[]{:S(2)}) async-start(bf16[128,16,256]{2,0,1:T(8,128)(2,1)} %bitcast.157), calls=%async_computation | async-start | bytes 2097152 | tf_op jit(solution)/shard_map/all_to_all | solution.py:76
  66.7 0.1 all-gather.3.cloned.1.call-start
  66.8 27.8 %all-to-all-done = bf16[128,16,256]{2,0,1:T(8,128)(2,1)S(1)} async-done(((bf16[128,16,256]{2,0,1:T(8,128)(2,1)}), bf16[128,16,256]{2,0,1:T(8,128)(2,1)S(1)}, u32[]{:S(2)}, u32[]{:S(2)}) %all-to-all-start) | async-done | bytes 1048608 | tf_op jit(solution)/shard_map/all_to_all | solution.py:76
  94.6 0.1 convert_reduce_fusion.1
  94.7 1.5 add_convert_fusion.4
  96.2 0.1 all-gather.3.cloned.1.call-update
  96.3 0.1 all-gather.5.cloned.1.call-start
  96.4 32.1 %all-gather.3.cloned.1.call-done = bf16[128,4096]{1,0:T(8,128)(2,1)} async-done(((bf16[128,256]{1,0:T(8,128)(2,1)}), bf16[128,4096]{1,0:T(8,128)(2,1)}) %all-gather.3.cloned.1.call-update) | async-done | bytes 1048592 | tf_op jit(solution)/shard_map/all_gather | solution.py:80
  128.4 1.5 fusion.23
  130.0 2.5 %fusion.110 = f32[128,256]{1,0:T(8,128)S(1)} fusion(bf16[2,4096,256]{2,1,0:T(8,128)(2,1)} %param.17, bf16[128,4096]{1,0:T(8,128)(2,1)} %all-gather.3.cloned.1.call-done, f32[4096]{0:T(1024)S(1)} %bitcast.168, f32[128]{0:T(128)S(1)} %add_rsqrt_fusion), kind=kOutput, calls=%fused_computation.86 | convolution fusion | flops 270598144 | bytes 3293696 | tf_op jit(solution)/shard_map/dot_general | solution.py:54
  132.5 0.7 reshape.239
  133.2 2.1 fusion.116
  135.3 0.1 reshape.237
  135.4 2.8 %fusion.113 = f32[128,256]{1,0:T(8,128)} fusion(bf16[2,4096,256]{2,1,0:T(8,128)(2,1)} %param.16, bf16[128,4096]{1,0:T(8,128)(2,1)S(1)} %copy-done.2, f32[4096]{0:T(1024)} %bitcast.166, f32[128]{0:T(128)S(1)} %add_rsqrt_fusion), kind=kOutput, calls=%fused_computation.87 | convolution fusion | flops 270598144 | bytes 3293696 | tf_op jit(solution)/shard_map/dot_general | solution.py:53
  138.1 1.0 reshape.238
  139.1 1.1 subtract_convert_fusion
  140.2 0.6 copy-done.3
  140.8 0.2 fusion.166
  141.0 3.5 %fusion.42 = f32[128,2,1,32]{3,2,1,0:T(1,128)} fusion(bf16[128,32,2,128]{3,2,1,0:T(2,128)(2,1)} %get-tuple-element.7, bf16[128,2,128,1]{2,1,0,3:T(2,128)(2,1)S(1)} %fusion.166), kind=kOutput, calls=%fused_computation.48 | convolution fusion | flops 2097152 | bytes 2195456 | tf_op jit(solution)/shard_map/bkgd,bskd->bkgs/dot_general | solution.py:32
  144.5 1.0 copy.31
  145.6 1.9 fusion.144
  147.5 0.9 copy.35
  148.4 0.1 fusion.155
  148.5 0.1 copy.36
  148.6 0.1 copy.17
  148.7 0.6 fusion.40
  149.4 0.2 add_convert_fusion.1
  149.6 5.0 %fusion.77 = f32[128,688]{0,1:T(8,128)} fusion(bf16[2,4096,688]{1,2,0:T(8,128)(2,1)} %param.19, bf16[128,4096]{1,0:T(8,128)(2,1)S(1)} %copy-done.2, f32[4096]{0:T(1024)} %bitcast.167, f32[128]{0:T(128)S(1)} %add_rsqrt_fusion), kind=kOutput, calls=%fused_computation.75 | convolution fusion | flops 723693568 | bytes 7053824 | tf_op jit(solution)/shard_map/dot_general | solution.py:58
  154.7 8.5 %fusion = f32[128,4096]{1,0:T(8,128)S(1)} fusion(bf16[2,688,4096]{2,1,0:T(8,128)(2,1)} %param.21, bf16[2,4096,688]{1,2,0:T(8,128)(2,1)} %param.20, f32[128,688]{0,1:T(8,128)} %fusion.77, bf16[128,4096]{1,0:T(8,128)(2,1)S(1)} %copy-done.2, f32[4096]{0:T(1024)S(1)} %bitcast.169, f32[128]{0:T(128)S(1)} %add_rsqrt_fusion), kind=kOutput, calls=%fused_computation | convolution fusion | flops 1445642240 | bytes 14787072 | tf_op jit(solution)/shard_map/dot_general | solution.py:61
  163.2 2.0 fusion.19
  165.3 0.1 copy.67
  165.4 32.5 %all_to_all.26 = bf16[128,16,256]{2,0,1:T(8,128)(2,1)S(1)} all-to-all(bf16[128,16,256]{2,0,1:T(8,128)(2,1)S(1)} %bitcast.158), channel_id=1, replica_groups=mesh['dp'=4,'tp'=16] {'tp'}, dimensions={1} | all-to-all | bytes 2097152 | tf_op jit(solution)/shard_map/all_to_all | solution.py:76
  197.9 0.1 convert_reduce_fusion
  198.0 0.7 add_convert_fusion
  198.7 0.1 all-gather.5.cloned.1.call-update
  198.7 31.9 %all-gather.5.cloned.1.call-done = bf16[128,4096]{1,0:T(8,128)(2,1)} async-done(((bf16[128,256]{1,0:T(8,128)(2,1)}), bf16[128,4096]{1,0:T(8,128)(2,1)}) %all-gather.5.cloned.1.call-update) | async-done | bytes 1048592 | tf_op jit(solution)/shard_map/all_gather | solution.py:80
  230.6 2.3 copy.70
  (39 shorter events, 0.3 us)
Async XLA Ops:
  9.3 4.1 %copy-start.12 = (f32[1,4096]{1,0:T(1,128)}, f32[1,4096]{1,0:T(1,128)S(1)}, u32[]{:S(2)}) copy-start(f32[1,4096]{1,0:T(1,128)S(1)} %get-tuple-element.22) | copy-start | bytes 49156
  10.8 2.6 %copy-start.1 = (bf16[128,4096]{1,0:T(8,128)(2,1)S(1)}, bf16[128,4096]{1,0:T(8,128)(2,1)}, u32[]{:S(2)}) copy-start(bf16[128,4096]{1,0:T(8,128)(2,1)} %param.12) | copy-start | bytes 3145732
  25.2 7.2 %copy-start.13 = (f32[1,4096]{1,0:T(1,128)S(1)}, f32[1,4096]{1,0:T(1,128)}, u32[]{:S(2)}) copy-start(f32[1,4096]{1,0:T(1,128)} %copy-done.12) | copy-start | bytes 49156
  36.2 5.2 %copy-start = (bf16[128,32,2,128]{3,2,1,0:T(2,128)(2,1)S(1)}, bf16[128,32,2,128]{3,2,1,0:T(2,128)(2,1)}, u32[]{:S(2)}) copy-start(bf16[128,32,2,128]{3,2,1,0:T(2,128)(2,1)} %get-tuple-element.6) | copy-start | bytes 6291460
  36.2 5.2 %copy-start.9 = (bf16[128,2,32,1]{2,3,1,0:T(2,128)(2,1)S(1)}, bf16[128,2,32,1]{2,3,1,0:T(2,128)(2,1)}, u32[]{:S(2)}) copy-start(bf16[128,2,32,1]{2,3,1,0:T(2,128)(2,1)} %copy.26) | copy-start | bytes 49156
  55.9 74.1 %copy-start.10 = (f32[1,4096]{1,0:T(1,128)S(1)}, f32[1,4096]{1,0:T(1,128)}, u32[]{:S(2)}) copy-start(f32[1,4096]{1,0:T(1,128)} %get-tuple-element.21) | copy-start | bytes 49156
  55.9 38.7 %all-to-all-start = ((bf16[128,16,256]{2,0,1:T(8,128)(2,1)}), bf16[128,16,256]{2,0,1:T(8,128)(2,1)S(1)}, u32[]{:S(2)}, u32[]{:S(2)}) async-start(bf16[128,16,256]{2,0,1:T(8,128)(2,1)} %bitcast.157), calls=%async_computation | async-start | bytes 2097152 | tf_op jit(solution)/shard_map/all_to_all | solution.py:76
  66.7 61.7 %all-gather.3.cloned.1.call-start = ((), (), s32[]{:S(2)}) async-start(), calls=%async_computation.2 | async-start | bytes 1114112 | tf_op jit(solution)/shard_map/all_gather | solution.py:80
  96.3 134.3 %all-gather.5.cloned.1.call-start = ((), (), s32[]{:S(2)}) async-start(), calls=%async_computation.3 | async-start | bytes 1114112 | tf_op jit(solution)/shard_map/all_gather | solution.py:80
  130.0 3.2 %copy-start.2 = (bf16[128,4096]{1,0:T(8,128)(2,1)S(1)}, bf16[128,4096]{1,0:T(8,128)(2,1)}, u32[]{:S(2)}) copy-start(bf16[128,4096]{1,0:T(8,128)(2,1)} %all-gather.3.cloned.1.call-done) | copy-start | bytes 3145732
  140.2 0.6 copy-start.3
  140.2 0.8 copy-start.5
  140.2 5.4 %copy-start.8 = (bf16[128,2,64]{2,1,0:T(2,128)(2,1)S(1)}, bf16[128,2,64]{2,1,0:T(2,128)(2,1)}, u32[]{:S(2)}) copy-start(bf16[128,2,64]{2,1,0:T(2,128)(2,1)} %get-tuple-element.9) | copy-start | bytes 98308
  141.0 4.5 %copy-start.4 = (bf16[128,2,64]{2,1,0:T(2,128)(2,1)S(1)}, bf16[128,2,64]{2,1,0:T(2,128)(2,1)}, u32[]{:S(2)}) copy-start(bf16[128,2,64]{2,1,0:T(2,128)(2,1)} %copy-done.3) | copy-start | bytes 98308
  141.0 4.5 %copy-start.6 = (bf16[128,2,64]{2,1,0:T(2,128)(2,1)S(1)}, bf16[128,2,64]{2,1,0:T(2,128)(2,1)}, u32[]{:S(2)}) copy-start(bf16[128,2,64]{2,1,0:T(2,128)(2,1)} %copy-done.5) | copy-start | bytes 98308
  144.5 4.9 %copy-start.7 = (f32[128,2,128]{2,1,0:T(2,128)S(1)}, f32[128,2,128]{2,1,0:T(2,128)}, u32[]{:S(2)}) copy-start(f32[128,2,128]{2,1,0:T(2,128)} %reshape.239) | copy-start | bytes 393220
  149.6 5.1 %copy-start.11 = (f32[1,4096]{1,0:T(1,128)S(1)}, f32[1,4096]{1,0:T(1,128)}, u32[]{:S(2)}) copy-start(f32[1,4096]{1,0:T(1,128)} %get-tuple-element.21) | copy-start | bytes 49156
Sparse Core Ops, SparseCore 0:
  96.4 31.9 all-gather.2
  198.8 31.6 all-gather.4
where the time goes:
time: 241 us; the launch traced here: 240 us
  waiting for transfers between devices  91.8 us (38%)
  matrix products  53.9 us (22%)
  blocking collectives  32.5 us (13%)
  local copies, waits for them, and re-layouts  23.2 us (10%)
  between operations  13.8 us (6%)
  other arithmetic  13.6 us (6%)
  starting transfers between devices  11 us (5%)
    all_gather x2, waiting for transfers between devices, per_device(): x_res = lax.all_gather(new_cols, 'tp', axis=1, tiled=True)  63.9 us
    all_to_all x1, blocking collectives, per_device(): received = lax.all_to_all(partial_sum, 'tp', 1, 0, tiled=True)  32.5 us
    all_to_all x1, waiting for transfers between devices, per_device(): received = lax.all_to_all(partial_sum, 'tp', 1, 0, tiled=True)  27.8 us
    dot_general x2, matrix products, layer_update(): jnp.dot(mlp_hidden, wd_layer, preferred_element_type=jnp.float32)  18.4 us
    all_to_all x1, starting transfers between devices, per_device(): received = lax.all_to_all(partial_sum, 'tp', 1, 0, tiled=True)  10.9 us
    dot_general x2, matrix products, layer_update(): jnp.dot(normed, wg_layer, preferred_element_type=jnp.float32)  10.2 us
    squeeze x1, local copies, waits for them, and re-layouts, per_device(): v_cache[layer_idx]  7.1 us
    squeeze x1, local copies, waits for them, and re-layouts, per_device(): k_cache[layer_idx]  5.95 us
  transfers between devices with their start and end apart: 3, of which 3 were waited for; matrix products, arithmetic and copies ran while one was open for 0% of the time, Pallas kernels for 0%

commit v1 on v0

v1 whole, which is shorter than its diff:
```python
import functools

import numpy as np
import jax
import jax.numpy as jnp
from jax import lax
from jax.experimental import pallas as pl
from jax.experimental.pallas import tpu as pltpu
from jax.sharding import PartitionSpec as P

NORM_EPS = 1e-5
ROPE_BASE = 500000.0
F32 = jnp.float32
BF16 = jnp.bfloat16
AHEAD = 6
NSUB = 2
LAG = 3


def decode_kernel(cfg, x_hbm, len_ref, freq_ref, gain_ref, wq_hbm, wk_hbm, wv_hbm, wo_hbm, wg_hbm, wu_hbm, wd_hbm,
                  kc_hbm, vc_hbm, out_hbm,
                  xg, wqkv, wg, wu, wod, kbuf, vbuf, gain_s, rb, lenb, cosb, sinb, acc_qkv, acc_g, acc_u, ut,
                  qs, ks, vs, logit_s, prob_s, hbuf, attn_s, own_f, snd_f, rcv_f, shr_snd, shr_rcv, stats,
                  x_sem, w_sem, kv_sem, od_sem, pair_s_sem, pair_r_sem, rs_s_sem, rs_r_sem, st_s_sem, st_r_sem,
                  ag_s_sem, ag_l_sem, ag_r_sem, pf_s_sem, pf_r_sem, out_sem):
    tp, rows, width, ff, seq, head, hq, layers = cfg
    chips = tp // 2
    half = chips // 2
    cw = width // tp
    me = lax.axis_index("tp")
    z = me // 2
    c = lax.rem(me, 2)
    partner = z * 2 + (1 - c)
    scale = head ** -0.5
    nch = tp
    nqkv = 3 * cw
    grp = 8
    ngrp = rows // grp
    gcols = grp * seq * hq

    def ring_dev(off):
        return lax.rem(z + off + chips, chips) * 2 + c

    def x_copy(k):
        return pltpu.make_async_copy(x_hbm.at[:, pl.ds(k * cw, cw)], xg.at[0, k], x_sem.at[k])

    def w_copies(l, k):
        r = pl.ds(k * cw, cw)
        return [
            pltpu.make_async_copy(wq_hbm.at[l, r, :], wqkv.at[k, :, 0:cw], w_sem.at[k, 0]),
            pltpu.make_async_copy(wk_hbm.at[l, r, :], wqkv.at[k, :, cw:2 * cw], w_sem.at[k, 1]),
            pltpu.make_async_copy(wv_hbm.at[l, r, :], wqkv.at[k, :, 2 * cw:3 * cw], w_sem.at[k, 2]),
            pltpu.make_async_copy(wg_hbm.at[l, :, r], wg.at[k], w_sem.at[k, 3]),
            pltpu.make_async_copy(wu_hbm.at[l, :, r], wu.at[k], w_sem.at[k, 4]),
        ]

    def kv_copies(l):
        return [pltpu.make_async_copy(kc_hbm.at[l], kbuf, kv_sem.at[0]), pltpu.make_async_copy(vc_hbm.at[l], vbuf, kv_sem.at[1])]

    def od_copies(l, j):
        cs = pl.ds(j * 2 * cw, 2 * cw)
        return [
            pltpu.make_async_copy(wo_hbm.at[l, :, cs], wod.at[j, 0:cw, :], od_sem.at[j, 0]),
            pltpu.make_async_copy(wd_hbm.at[l, :, cs], wod.at[j, cw:cw + ff, :], od_sem.at[j, 1]),
        ]

    def start(cps):
        for cp in cps:
            cp.start()

    def wait(cps):
        for cp in cps:
            cp.wait()

    sends = []

    def send(src, dst, s_sem, r_sem, dev):
        cp = pltpu.make_async_remote_copy(src_ref=src, dst_ref=dst, send_sem=s_sem, recv_sem=r_sem,
                                          device_id={"tp": dev}, device_id_type=pl.DeviceIdType.MESH)
        cp.start()
        sends.append(cp)

    def wait_recv(dst, r_sem):
        pltpu.make_async_remote_copy(src_ref=dst, dst_ref=dst, send_sem=r_sem, recv_sem=r_sem, device_id={"tp": partner}, device_id_type=pl.DeviceIdType.MESH).wait_recv()

    for k in range(nch):
        x_copy(k).start()
    for k in range(AHEAD):
        start(w_copies(0, k))

    barrier = pltpu.get_barrier_semaphore()
    for d in range(1, tp):
        pl.semaphore_signal(barrier, inc=1, device_id={"tp": lax.rem(me + d, tp)}, device_id_type=pl.DeviceIdType.MESH)

    pad = wod.shape[1] - cw - ff
    if pad:
        for j in range(chips):
            wod[j, cw + ff:, :] = jnp.zeros((pad, 2 * cw), BF16)
        ut[ff:, :] = jnp.zeros((pad, rows), F32)
    gain_s[...] = gain_ref[...].astype(F32)
    lenb[...] = jnp.broadcast_to(len_ref[...].astype(F32), (rows, rows)).T
    ang = lenb[...] * freq_ref[...]
    lane = lax.broadcasted_iota(jnp.int32, (rows, head), 1)
    cosb[...] = jnp.cos(ang)
    sn = jnp.sin(ang)
    sinb[...] = jnp.where(lane < head // 2, -sn, sn)

    def set_inv_rms(ssq):
        inv = lax.rsqrt(ssq / width + NORM_EPS)
        rb[...] = jnp.broadcast_to(inv, rb.shape)

    def do_chunk(l, k):
        xk = xg[l, k].astype(F32)
        g = gain_s[l:l + 1, pl.ds(pl.multiple_of(k * cw, cw), cw)]
        a = (xk * rb[...] * g).astype(BF16)
        acc_qkv[...] += jnp.dot(a, wqkv[k], preferred_element_type=F32)
        nt = (((1,), (1,)), ((), ()))
        acc_g[...] += lax.dot_general(wg[k], a, nt, preferred_element_type=F32)
        acc_u[...] += lax.dot_general(wu[k], a, nt, preferred_element_type=F32)

    def rope(v):
        return (v * cosb[...] + pltpu.roll(v, head // 2, 1) * sinb[...]).astype(BF16).astype(F32)

    def zero_acc():
        acc_qkv[...] = jnp.zeros_like(acc_qkv)
        acc_g[...] = jnp.zeros_like(acc_g)
        acc_u[...] = jnp.zeros_like(acc_u)

    def attention(l):
        for h in range(hq):
            q = acc_qkv[:, h * head:(h + 1) * head].astype(BF16).astype(F32)
            k = acc_qkv[:, cw + h * head:cw + (h + 1) * head].astype(BF16).astype(F32)
            v = acc_qkv[:, 2 * cw + h * head:2 * cw + (h + 1) * head].astype(BF16).astype(F32)
            qs[:, h] = rope(q).reshape(ngrp, grp, head)
            ks[:, h] = rope(k).reshape(ngrp, grp, head)
            vs[:, h] = v.reshape(ngrp, grp, head)
        wait(kv_copies(l))
        m = hq * grp
        for g in range(ngrp):
            q = qs[g].reshape(m, head).astype(BF16)
            kk = kbuf[g * gcols:(g + 1) * gcols, :]
            logit_s[g * m:(g + 1) * m, :] = lax.dot_general(q, kk, (((1,), (1,)), ((), ())), preferred_element_type=F32)
        col = lax.broadcasted_iota(jnp.int32, (m, gcols), 1)
        row = lax.broadcasted_iota(jnp.int32, (m, gcols), 0)
        same = ((col // (seq * hq)) == lax.rem(row, grp)) & (lax.rem(col, hq) == row // grp)
        key = jnp.where(same, lax.rem(col // hq, seq), 2 * seq).astype(F32)
        for g in range(ngrp):
            ln = lenb[g * grp:(g + 1) * grp, 0:1]
            ln = jnp.concatenate([ln] * hq, axis=0)
            lg = jnp.where(key < ln, logit_s[g * m:(g + 1) * m, :] * scale, -jnp.inf)
            qv = qs[g].reshape(m, head)
            kv = ks[g].reshape(m, head)
            vv = vs[g].reshape(m, head)
            sl = jnp.sum(qv * kv, axis=1, keepdims=True) * scale
            peak = jnp.maximum(jnp.max(lg, axis=1, keepdims=True), sl)
            w = jnp.exp(lg - peak)
            sw = jnp.exp(sl - peak)
            den = jnp.sum(w, axis=1, keepdims=True) + sw
            prob_s[g * m:(g + 1) * m, :] = (w / den).astype(BF16)
            sp = (sw / den).astype(BF16).astype(F32)
            vs[g] = (sp * vv).reshape(hq, grp, head)
        for g in range(ngrp):
            p = prob_s[g * m:(g + 1) * m, :]
            o = jnp.dot(p, vbuf[g * gcols:(g + 1) * gcols, :], preferred_element_type=F32)
            o = o + vs[g].reshape(m, head)
            for h in range(hq):
                attn_s[g * grp:(g + 1) * grp, h * head:(h + 1) * head] = o[h * grp:(h + 1) * grp]
        hbuf[:, 0:cw] = attn_s[...].astype(BF16)

    def mlp_act():
        gt = acc_g[...].astype(BF16).astype(F32)
        up = acc_u[...].astype(BF16).astype(F32)
        ut[0:ff, :] = gt * (1.0 / (1.0 + jnp.exp(-gt))) * up
        for i in range(ut.shape[0] // 128):
            hbuf[:, cw + i * 128:cw + (i + 1) * 128] = ut[i * 128:(i + 1) * 128, :].T.astype(BF16)

    offs = [half]
    for d in range(half - 1, 0, -1):
        offs += [d, chips - d]
    offs += [0]

    def out_proj(l):
        hv = hbuf[...]

        def finish(i):
            off = offs[i]
            wait_recv(rcv_f.at[l, i], pair_r_sem.at[l, i])
            s = own_f[l, i] + rcv_f[l, i]
            if off == 0:
                own_f[l, i] = s
            else:
                shr_snd[l, i] = s.astype(BF16)
                send(shr_snd.at[l, i], shr_rcv.at[l, i], rs_s_sem.at[l, i], rs_r_sem.at[l, i], ring_dev(off))

        for i in range(chips):
            j = lax.rem(z + offs[i], chips)
            wait(od_copies(l, j))
            p = jnp.dot(hv, wod[j], preferred_element_type=F32)
            lo, hi = p[:, :cw], p[:, cw:]
            own_f[l, i] = jnp.where(c == 0, lo, hi)
            snd_f[l, i] = jnp.where(c == 0, hi, lo)
            send(snd_f.at[l, i], rcv_f.at[l, i], pair_s_sem.at[l, i], pair_r_sem.at[l, i], partner)
            if i >= LAG:
                finish(i - LAG)
        for i in range(chips - LAG, chips):
            finish(i)

    def reduce_own(l):
        acc = xg[l, me].astype(F32) + own_f[l, chips - 1]
        for i in range(chips - 1):
            wait_recv(shr_rcv.at[l, i], rs_r_sem.at[l, i])
            acc = acc + shr_rcv[l, i].astype(F32)
        return acc.astype(BF16)

    pr = rows // NSUB

    def gather(l, use):
        dst = l + 1

        def piece(src, p):
            return xg.at[dst, src, pl.ds(p * pr, pr), :]

        def to_partner(src, q, p):
            send(piece(src, p), piece(src, p), pf_s_sem.at[l, q, p], pf_r_sem.at[l, q, p], partner)

        def ring(src, step, p, right):
            dev = ring_dev(1 if right else -1)
            r = (ag_l_sem if right else ag_r_sem).at[l, step, p]
            send(piece(src, p), piece(src, p), ag_s_sem.at[l, step, 0 if right else 1, p], r, dev)

        for p in range(NSUB):
            ring(me, 0, p, True)
            ring(me, 0, p, False)
        for p in range(NSUB):
            to_partner(me, 0, p)
        use("own", [me])
        for s in range(1, half):
            sl, sr = ring_dev(-s), ring_dev(s)
            for p in range(NSUB):
                wait_recv(piece(sl, p), ag_l_sem.at[l, s - 1, p])
                if s < half - 1 or p < NSUB // 2:
                    ring(sl, s, p, True)
                to_partner(sl, 2 * s - 1, p)
                wait_recv(piece(sr, p), ag_r_sem.at[l, s - 1, p])
                if s < half - 1 or p >= NSUB // 2:
                    ring(sr, s, p, False)
                to_partner(sr, 2 * s, p)
            use("ring", [sl, sr])
            flip = 1 - 2 * c
            qs_ = [0] if s == 1 else [2 * s - 3, 2 * s - 2]
            srcs = [me + flip] if s == 1 else [ring_dev(1 - s) + flip, ring_dev(s - 1) + flip]
            for q, src in zip(qs_, srcs):
                for p in range(NSUB):
                    wait_recv(piece(src, p), pf_r_sem.at[l, q, p])
            use("pair", srcs)
        far = ring_dev(half)
        for p in range(NSUB // 2):
            wait_recv(piece(far, p), ag_l_sem.at[l, half - 1, p])
            to_partner(far, 2 * half - 1, p)
            p2 = p + NSUB // 2
            wait_recv(piece(far, p2), ag_r_sem.at[l, half - 1, p2])
            to_partner(far, 2 * half - 1, p2)
        use("ring", [far])
        flip = 1 - 2 * c
        for q, src in ((2 * half - 3, ring_dev(1 - half) + flip), (2 * half - 2, ring_dev(half - 1) + flip), (2 * half - 1, far + flip)):
            for p in range(NSUB):
                wait_recv(piece(src, p), pf_r_sem.at[l, q, p])
            use("pair", [src])

    ssq = jnp.zeros((rows, cw), F32)
    for k in range(nch):
        x_copy(k).wait()
        xf = xg[0, k].astype(F32)
        ssq = ssq + xf * xf
    set_inv_rms(jnp.sum(ssq, axis=1, keepdims=True))
    zero_acc()

    def l0_body(k, carry):
        wait(w_copies(0, k))
        do_chunk(0, k)

        @pl.when(k + AHEAD < nch)
        def _():
            start(w_copies(0, k + AHEAD))

        @pl.when(k + AHEAD == nch)
        def _():
            start(kv_copies(0))
            for i in range(chips):
                start(od_copies(0, lax.rem(z + offs[i], chips)))
        return carry

    lax.fori_loop(0, nch, l0_body, 0)

    for l in range(layers):
        attention(l)
        mlp_act()
        if l == 0:
            pl.semaphore_wait(barrier, tp - 1)
        out_proj(l)
        if l + 1 < layers:
            for k in range(nch):
                start(w_copies(l + 1, k))
            start(kv_copies(l + 1))
            for i in range(chips):
                start(od_copies(l + 1, lax.rem(z + offs[i], chips)))
        xn = reduce_own(l)
        xg[l + 1, me] = xn
        if l + 1 < layers:
            xf = xn.astype(F32)
            sq = jnp.sum(xf * xf, axis=1, keepdims=True)
            stats[l, me] = jnp.broadcast_to(sq, (rows, rows)).T[0:8, :]

            def use(kind, srcs, l=l):
                if kind == "own":
                    for d in range(1, tp):
                        send(stats.at[l, me], stats.at[l, me], st_s_sem.at[l, d], st_r_sem.at[l, me], lax.rem(me + d, tp))
                    zero_acc()
                    wait_all_w = w_copies
                    return
                if kind == "ring" and not use.ready:
                    use.ready = True
                    for d in range(1, tp):
                        o = lax.rem(me + d, tp)
                        wait_recv(stats.at[l, o], st_r_sem.at[l, o])
                    tot = stats[l, 0]
                    for d in range(1, tp):
                        tot = tot + stats[l, d]
                    set_inv_rms(jnp.broadcast_to(tot[0:1, :], (rows, rows)).T[:, 0:1])
                    srcs = [me] + srcs
                for src in srcs:
                    wait(w_copies(l + 1, src))
                    do_chunk(l + 1, src)

            use.ready = False
            gather(l, use)
        else:
            outs = []

            def use_out(kind, srcs, l=l):
                for src in srcs:
                    cp = pltpu.make_async_copy(xg.at[l + 1, src], out_hbm.at[:, pl.ds(pl.multiple_of(src * cw, cw), cw)], out_sem.at[src])
                    cp.start()
                    outs.append(cp)

            gather(l, use_out)
            wait(outs)
    for cp in sends:
        cp.wait_send()


def solution(mesh):
    tp = mesh.shape["tp"]
    arg_specs = (P("dp", None), P("dp"), P(), P(None, None, "tp"), P(None, None, "tp"), P(None, None, "tp"), P(None, "tp", None),
                 P(None, None, "tp"), P(None, None, "tp"), P(None, "tp", None), P(None, "dp", None, "tp", None), P(None, "dp", None, "tp", None))

    def per_device(x_in, lengths, norm_gain, w_q, w_k, w_v, w_o, w_gate, w_up, w_down, k_cache, v_cache):
        rows, width = x_in.shape
        layers, _, seq, hq, head = k_cache.shape
        ff = w_gate.shape[2]
        cw = width // tp
        chips = tp // 2
        assert w_q.shape[2] == cw == hq * head
        freq = (1.0 / (np.float32(ROPE_BASE) ** (np.arange(0, head, 2).astype(np.float32) / np.float32(head)))).astype(np.float32)
        freq = jnp.asarray(np.concatenate([freq, freq])[None, :])
        ffp = -(-(cw + ff) // 256) * 256 - cw
        kvr = rows * seq * hq
        ngrp = rows // 8
        m = hq * 8
        any_spec = pl.BlockSpec(memory_space=pl.ANY)
        vmem = pl.BlockSpec(memory_space=pltpu.VMEM)
        V = pltpu.VMEM
        D = pltpu.SemaphoreType.DMA
        scratch = [
            V((layers + 1, tp, rows, cw), BF16),
            V((tp, cw, 3 * cw), BF16),
            V((tp, ff, cw), BF16), V((tp, ff, cw), BF16),
            V((chips, cw + ffp, 2 * cw), BF16),
            V((kvr, head), BF16), V((kvr, head), BF16),
            V((layers, width), F32),
            V((rows, cw), F32),
            V((rows, rows), F32),
            V((rows, head), F32), V((rows, head), F32),
            V((rows, 3 * cw), F32),
            V((ff, rows), F32), V((ff, rows), F32),
            V((ffp, rows), F32),
            V((ngrp, hq, 8, head), F32), V((ngrp, hq, 8, head), F32), V((ngrp, hq, 8, head), F32),
            V((rows * hq, 8 * seq * hq), F32),
            V((rows * hq, 8 * seq * hq), BF16),
            V((rows, cw + ffp), BF16),
            V((rows, cw), F32),
            V((layers, chips, rows, cw), F32),
            V((layers, chips, rows, cw), F32),
            V((layers, chips, rows, cw), F32),
            V((layers, chips, rows, cw), BF16),
            V((layers, chips, rows, cw), BF16),
            V((layers, tp, 8, rows), F32),
            D((tp,)), D((tp, 5)), D((2,)), D((chips, 2)),
            D((layers, chips)), D((layers, chips)), D((layers, chips)), D((layers, chips)),
            D((layers, tp)), D((layers, tp)),
            D((layers, chips // 2, 2, NSUB)), D((layers, chips // 2, NSUB)), D((layers, chips // 2, NSUB)),
            D((layers, chips, NSUB)), D((layers, chips, NSUB)), D((tp,)),
        ]
        cfg = (tp, rows, width, ff, seq, head, hq, layers)
        return pl.pallas_call(
            functools.partial(decode_kernel, cfg),
            out_shape=jax.ShapeDtypeStruct((rows, width), BF16),
            in_specs=[any_spec, vmem, vmem, vmem] + [any_spec] * 9,
            out_specs=any_spec,
            scratch_shapes=scratch,
            compiler_params=pltpu.CompilerParams(collective_id=0, has_side_effects=True, vmem_limit_bytes=60 * 1024 * 1024),
        )(x_in, lengths.reshape(1, rows), freq, norm_gain, w_q, w_k, w_v, w_o, jnp.swapaxes(w_gate, 1, 2), jnp.swapaxes(w_up, 1, 2), w_down,
          k_cache.reshape(layers, kvr, head), v_cache.reshape(layers, kvr, head))

    return jax.shard_map(per_device, mesh=mesh, in_specs=arg_specs, out_specs=P("dp", None), check_vma=False)
```

time: 241 us -> 90.3 us (0.37)
  waiting for transfers between devices: 91.8 us -> 0 us
  Pallas kernels: 0 us -> 87.9 us
  matrix products: 53.9 us -> 0 us
  blocking collectives: 32.5 us -> 0 us
  local copies, waits for them, and re-layouts: 23.2 us -> 2.29 us
  between operations: 13.8 us -> 0.01 us
  other arithmetic: 13.6 us -> 0 us
  starting transfers between devices: 11 us -> 0 us
    pallas_call x0 -> x1, Pallas kernels: none -> 87.9 us  [per_device(): pl.pallas_call(functools.partial(decode_kernel, cfg), out_shape=jax.Shape...]
    all_gather x2 -> x0, waiting for transfers between devices: 63.9 us -> none  [per_device(): x_res = lax.all_gather(new_cols, 'tp', axis=1, tiled=True)]
    dot_general x16 -> x0, matrix products: 53.9 us -> none  [the longest x2 18.4 us: layer_update(): jnp.dot(mlp_hidden, wd_layer, preferred_element_type=jnp.float32)]
    all_to_all x1 -> x0, blocking collectives: 32.5 us -> none  [per_device(): received = lax.all_to_all(partial_sum, 'tp', 1, 0, tiled=True)]
    all_to_all x1 -> x0, waiting for transfers between devices: 27.8 us -> none  [per_device(): received = lax.all_to_all(partial_sum, 'tp', 1, 0, tiled=True)]
    squeeze x2 -> x0, local copies, waits for them, and re-layouts: 13 us -> none  [the longest x1 7.1 us: per_device(): v_cache[layer_idx]]
    all_to_all x1 -> x0, starting transfers between devices: 10.9 us -> none  [per_device(): received = lax.all_to_all(partial_sum, 'tp', 1, 0, tiled=True)]
    convert_element_type x10 -> x0, local copies, waits for them, and re-layouts: 4 us -> none  [the longest x2 1.68 us: decode_attention(): v_new.astype(jnp.float32)[:, :, None, :]]
  transfers between devices with their start and end apart: 3 -> 0, of which waited for: 3 -> 0; matrix products, arithmetic and copies ran while one was open for 0% -> 0% of each run, Pallas kernels for 0% -> 0%
where the time goes in v1:
time: 90.3 us; the launch traced here: 90.2 us
  Pallas kernels  87.9 us (97%)
  local copies, waits for them, and re-layouts  2.29 us (3%)
    pallas_call x1, Pallas kernels, per_device(): pl.pallas_call(functools.partial(decode_kernel, cfg), out_shape=jax.Shape...  87.9 us
    unnamed x1, local copies, waits for them, and re-layouts  2.29 us

profile of v1, /device:TPU:21, one launch (start us, length us, event | category | flops | bytes accessed | tf_op | source)
XLA Modules:
  0.0 90.2 jit_solution(16470568732731448230)
XLA Ops:
  0.0 87.9 %shard_map.127 = bf16[128,4096]{1,0:T(8,128)(2,1)} custom-call(bf16[128,4096]{1,0:T(8,128)(2,1)} %x_hbm.1, s32[1,128]{1,0:T(1,128)} %bitcast.9, f32[1,128]{1,0:T(1,128)} %constant.2.clone.freq_ref, bf16[2,4096]{1,0:T(2,128)(2,1)} %gain_ref.1, bf16[2,4096,256]{2,1,0:T(8,128)(2,1)} %wq_hbm.1, bf16[2,4096,256]{2,1,0:T(8,128)(2,1)} %wk_hbm.1, ...), custom_call_target="tpu_custom_call" | custom-call | tf_op jit(solution)/shard_map/pallas_call | solution.py:405
  87.9 2.3 %copy.15 = bf16[128,4096]{1,0:T(8,128)(2,1)} copy(bf16[128,4096]{1,0:T(8,128)(2,1)} %shard_map.127) | data formatting | bytes 2097152

commit v2 on v1

v2 whole, which is shorter than its diff:
```python
import functools

import numpy as np
import jax
import jax.numpy as jnp
from jax import lax
from jax.experimental import pallas as pl
from jax.experimental.pallas import tpu as pltpu
from jax.sharding import PartitionSpec as P

NORM_EPS = 1e-5
ROPE_BASE = 500000.0
F32 = jnp.float32
BF16 = jnp.bfloat16
NSUB = 2
LAG = 3
FIRST = 2
AHEAD = 7
RING = 8


def decode_kernel(cfg, x_hbm, len_ref, freq_ref, gain_ref, wq_hbm, wk_hbm, wv_hbm, wo_hbm, wg_hbm, wu_hbm, wd_hbm,
                  kc_hbm, vc_hbm, out_hbm,
                  xg, wqkv, wgu, wod, kbuf, vbuf, gain_s, rb, lenb, cosb, sinb, acc_qkv, acc_g, acc_u, ut,
                  qs, ks, vs, logit_s, prob_s, hbuf, attn_s, own_f, snd_f, rcv_f, shr_snd, shr_rcv, stats,
                  x_sem, w_sem, wl_sem, kv_sem, od_sem, pair_s_sem, pair_r_sem, rs_s_sem, rs_r_sem, st_s_sem, st_r_sem,
                  ag_s_sem, ag_r_sem, pf_r_sem, out_sem):
    tp, rows, width, ff, seq, head, hq, layers = cfg
    chips = tp // 2
    half = chips // 2
    cw = width // tp
    me = lax.axis_index("tp")
    z = me // 2
    c = lax.rem(me, 2)
    partner = z * 2 + (1 - c)
    scale = head ** -0.5
    nch = tp
    nqkv = 3 * cw
    grp = 8
    ngrp = rows // grp
    gcols = grp * seq * hq

    def ring_dev(off):
        return lax.rem(z + off + chips, chips) * 2 + c

    def x_copy(k):
        return pltpu.make_async_copy(x_hbm.at[:, pl.ds(k * cw, cw)], xg.at[0, k], x_sem)

    def start_w(l, k, qkv_sem, gu_sem):
        r = pl.ds(k * cw, cw)
        for i, w in enumerate((wq_hbm, wk_hbm, wv_hbm)):
            pltpu.make_async_copy(w.at[l, r, :], wqkv.at[k, :, i * cw:(i + 1) * cw], qkv_sem).start()
        for i, w in enumerate((wg_hbm, wu_hbm)):
            pltpu.make_async_copy(w.at[l, :, r], wgu.at[k, i], gu_sem).start()

    def start_kv(l):
        pltpu.make_async_copy(kc_hbm.at[l], kbuf, kv_sem.at[0]).start()
        pltpu.make_async_copy(vc_hbm.at[l], vbuf, kv_sem.at[1]).start()

    def start_od(l, j):
        cs = pl.ds(j * 2 * cw, 2 * cw)
        pltpu.make_async_copy(wo_hbm.at[l, :, cs], wod.at[j, 0:cw, :], od_sem).start()
        pltpu.make_async_copy(wd_hbm.at[l, :, cs], wod.at[j, cw:cw + ff, :], od_sem).start()

    def start_all_od(l):
        for i in range(chips):
            start_od(l, lax.rem(z + offs[i], chips))

    def arrive(ref, sem):
        pltpu.make_async_copy(ref, ref, sem).wait()

    def send(src, dst, s_sem, r_sem, dev):
        cp = pltpu.make_async_remote_copy(src_ref=src, dst_ref=dst, send_sem=s_sem, recv_sem=r_sem,
                                          device_id={"tp": dev}, device_id_type=pl.DeviceIdType.MESH)
        cp.start()

    def wait_remote(dst, sem):
        return pltpu.make_async_remote_copy(src_ref=dst, dst_ref=dst, send_sem=sem, recv_sem=sem,
                                            device_id={"tp": partner}, device_id_type=pl.DeviceIdType.MESH)

    def wait_recv(dst, sem):
        wait_remote(dst, sem).wait_recv()

    def wait_sent(src, sem):
        wait_remote(src, sem).wait_send()

    offs = [half]
    for d in range(half - 1, 0, -1):
        offs += [d, chips - d]
    offs += [0]
    for k in range(nch):
        x_copy(k).start()
    for k in range(FIRST):
        start_w(0, k, w_sem.at[k, 0], w_sem.at[k, 1])

    scope_pre = jax.named_scope("pre")
    scope_pre.__enter__()
    barrier = pltpu.get_barrier_semaphore()
    for d in range(1, tp):
        pl.semaphore_signal(barrier, inc=1, device_id={"tp": lax.rem(me + d, tp)}, device_id_type=pl.DeviceIdType.MESH)

    pad = wod.shape[1] - cw - ff
    if pad:
        for j in range(chips):
            wod[j, cw + ff:, :] = jnp.zeros((pad, 2 * cw), BF16)
        ut[ff:, :] = jnp.zeros((pad, rows), F32)
    gain_s[...] = gain_ref[...].astype(F32)
    lenb[...] = jnp.broadcast_to(len_ref[...].astype(F32), (rows, rows)).T
    ang = lenb[...] * freq_ref[...]
    lane = lax.broadcasted_iota(jnp.int32, (rows, head), 1)
    cosb[...] = jnp.cos(ang)
    sn = jnp.sin(ang)
    sinb[...] = jnp.where(lane < head // 2, -sn, sn)
    scope_pre.__exit__(None, None, None)

    def set_inv_rms(ssq):
        inv = lax.rsqrt(ssq / width + NORM_EPS)
        rb[...] = jnp.broadcast_to(inv, rb.shape)

    def do_chunk(l, k):
        xk = xg[l, k].astype(F32)
        g = gain_s[l:l + 1, pl.ds(pl.multiple_of(k * cw, cw), cw)]
        a = (xk * rb[...] * g).astype(BF16)
        acc_qkv[...] += jnp.dot(a, wqkv[k], preferred_element_type=F32)
        nt = (((1,), (1,)), ((), ()))
        acc_g[...] += lax.dot_general(wgu[k, 0], a, nt, preferred_element_type=F32)
        acc_u[...] += lax.dot_general(wgu[k, 1], a, nt, preferred_element_type=F32)

    def rope(v):
        return (v * cosb[...] + pltpu.roll(v, head // 2, 1) * sinb[...]).astype(BF16).astype(F32)

    def zero_acc():
        acc_qkv[...] = jnp.zeros_like(acc_qkv)
        acc_g[...] = jnp.zeros_like(acc_g)
        acc_u[...] = jnp.zeros_like(acc_u)

    def attention(l):
        for h in range(hq):
            q = acc_qkv[:, h * head:(h + 1) * head].astype(BF16).astype(F32)
            k = acc_qkv[:, cw + h * head:cw + (h + 1) * head].astype(BF16).astype(F32)
            v = acc_qkv[:, 2 * cw + h * head:2 * cw + (h + 1) * head].astype(BF16).astype(F32)
            qs[:, h] = rope(q).reshape(ngrp, grp, head)
            ks[:, h] = rope(k).reshape(ngrp, grp, head)
            vs[:, h] = v.reshape(ngrp, grp, head)
        with jax.named_scope(f"kvwait{l}"):
            arrive(kbuf, kv_sem.at[0])
            arrive(vbuf, kv_sem.at[1])
        m = hq * grp
        for g in range(ngrp):
            q = qs[g].reshape(m, head).astype(BF16)
            kk = kbuf[g * gcols:(g + 1) * gcols, :]
            logit_s[g * m:(g + 1) * m, :] = lax.dot_general(q, kk, (((1,), (1,)), ((), ())), preferred_element_type=F32)
        col = lax.broadcasted_iota(jnp.int32, (m, gcols), 1)
        row = lax.broadcasted_iota(jnp.int32, (m, gcols), 0)
        same = ((col // (seq * hq)) == lax.rem(row, grp)) & (lax.rem(col, hq) == row // grp)
        key = jnp.where(same, lax.rem(col // hq, seq), 2 * seq).astype(F32)
        for g in range(ngrp):
            ln = lenb[g * grp:(g + 1) * grp, 0:1]
            ln = jnp.concatenate([ln] * hq, axis=0)
            lg = jnp.where(key < ln, logit_s[g * m:(g + 1) * m, :] * scale, -jnp.inf)
            qv = qs[g].reshape(m, head)
            kv = ks[g].reshape(m, head)
            vv = vs[g].reshape(m, head)
            sl = jnp.sum(qv * kv, axis=1, keepdims=True) * scale
            peak = jnp.maximum(jnp.max(lg, axis=1, keepdims=True), sl)
            w = jnp.exp(lg - peak)
            sw = jnp.exp(sl - peak)
            den = jnp.sum(w, axis=1, keepdims=True) + sw
            prob_s[g * m:(g + 1) * m, :] = (w / den).astype(BF16)
            sp = (sw / den).astype(BF16).astype(F32)
            vs[g] = (sp * vv).reshape(hq, grp, head)
        for g in range(ngrp):
            p = prob_s[g * m:(g + 1) * m, :]
            o = jnp.dot(p, vbuf[g * gcols:(g + 1) * gcols, :], preferred_element_type=F32)
            o = o + vs[g].reshape(m, head)
            for h in range(hq):
                attn_s[g * grp:(g + 1) * grp, h * head:(h + 1) * head] = o[h * grp:(h + 1) * grp]
        hbuf[:, 0:cw] = attn_s[...].astype(BF16)

    def mlp_act():
        gt = acc_g[...].astype(BF16).astype(F32)
        up = acc_u[...].astype(BF16).astype(F32)
        ut[0:ff, :] = gt * (1.0 / (1.0 + jnp.exp(-gt))) * up
        for i in range(ut.shape[0] // 128):
            hbuf[:, cw + i * 128:cw + (i + 1) * 128] = ut[i * 128:(i + 1) * 128, :].T.astype(BF16)

    def out_proj(l):
        arrive(wod.at[:, 0:cw + ff, :], od_sem)
        hv = hbuf[...]

        def finish(i):
            off = offs[i]
            wait_recv(rcv_f.at[l, i], pair_r_sem.at[i])
            s = own_f[l, i] + rcv_f[l, i]
            if off == 0:
                own_f[l, i] = s
            else:
                shr_snd[l, i] = s.astype(BF16)
                send(shr_snd.at[l, i], shr_rcv.at[l, i], rs_s_sem, rs_r_sem.at[i], ring_dev(off))

        for i in range(chips):
            j = lax.rem(z + offs[i], chips)
            p = jnp.dot(hv, wod[j], preferred_element_type=F32)
            lo, hi = p[:, :cw], p[:, cw:]
            own_f[l, i] = jnp.where(c == 0, lo, hi)
            snd_f[l, i] = jnp.where(c == 0, hi, lo)
            send(snd_f.at[l, i], rcv_f.at[l, i], pair_s_sem, pair_r_sem.at[i], partner)
            if i >= LAG:
                finish(i - LAG)
        for i in range(chips - LAG, chips):
            finish(i)
        wait_sent(snd_f.at[l], pair_s_sem)

    def reduce_own(l):
        acc = xg[l, me].astype(F32) + own_f[l, chips - 1]
        for i in range(chips - 1):
            wait_recv(shr_rcv.at[l, i], rs_r_sem.at[i])
            acc = acc + shr_rcv[l, i].astype(F32)
        wait_sent(shr_snd.at[l, 0:chips - 1], rs_s_sem)
        return acc.astype(BF16)

    pr = rows // NSUB

    def gather(l, use):
        dst = l + 1
        flip = 1 - 2 * c
        first, last = list(range(NSUB)), list(range(NSUB))[::-1]

        def piece(src, p):
            return xg.at[dst, src, pl.ds(p * pr, pr), :]

        def whole(src):
            return xg.at[dst, src]

        def slot(d, side):
            return 0 if d == 0 else (2 * half - 1 if d == half else 2 * d - 1 + side)

        def sem_of(d, side, p):
            return ag_r_sem.at[p * 2 + side] if d == 2 else ag_r_sem.at[2 * NSUB + (0 if d == half else (d // 2 + 1) * 2 - 1 + side)]

        def to_partner(ref, d, side):
            send(ref, ref, ag_s_sem, pf_r_sem.at[slot(d, side)], partner)

        def ring(ref, d, p, hops):
            send(ref, ref, ag_s_sem, sem_of(d, 0 if hops > 0 else 1, p), ring_dev(hops))

        def arrived(d, side):
            src = ring_dev(-d if side == 0 else d)
            wait_recv(whole(src), sem_of(d, side, 0))
            to_partner(whole(src), d, side)
            return src

        def from_partner(d, side):
            src = me + flip if d == 0 else ring_dev(-d if side == 0 else d) + flip
            wait_recv(whole(src), pf_r_sem.at[slot(d, side)])
            return src

        for i in range(NSUB):
            ring(piece(me, first[i]), 2, first[i], 2)
            ring(piece(me, last[i]), 2, last[i], -2)
        use("early", [])
        ring(whole(me), 1, 0, 1)
        ring(whole(me), 1, 0, -1)
        to_partner(whole(me), 0, 0)
        use("own", [me])
        two = [ring_dev(-2), ring_dev(2)]
        for i in range(NSUB):
            for side, p in ((0, first[i]), (1, last[i])):
                src = two[side]
                wait_recv(piece(src, p), sem_of(2, side, p))
                sg = 1 if side == 0 else -1
                if i < NSUB // 2:
                    ring(piece(src, p), 4, p, 2 * sg)
                ring(piece(src, p), 3, p, sg)
                to_partner(piece(src, p), 2, side)
        one = [arrived(1, 0), arrived(1, 1)]
        use("ring", two + one)
        use("pair", [from_partner(0, 0), from_partner(2, 0), from_partner(2, 1)])
        three = [arrived(3, 0), arrived(3, 1)]
        far = [arrived(4, 0)]
        use("pair", [from_partner(1, 0), from_partner(1, 1)])
        use("ring", three + far)
        for d, side in ((3, 0), (3, 1), (4, 0)):
            use("pair", [from_partner(d, side)])
        wait_sent(xg.at[dst, 0:7 + 2 * half], ag_s_sem)

    with jax.named_scope("stats"):
        ssq = jnp.zeros((rows, cw), F32)
        arrive(xg.at[0], x_sem)
        for k in range(FIRST, AHEAD):
            start_w(0, k, w_sem.at[k, 0], w_sem.at[k, 1])
        for k in range(nch):
            xf = xg[0, k].astype(F32)
            ssq = ssq + xf * xf
        set_inv_rms(jnp.sum(ssq, axis=1, keepdims=True))
        zero_acc()

    def l0_body(k, carry):
        b = lax.rem(k, RING)
        arrive(wqkv.at[k], w_sem.at[b, 0])
        arrive(wgu.at[k], w_sem.at[b, 1])
        do_chunk(0, k)

        @pl.when(k + AHEAD < nch)
        def _():
            nb = lax.rem(k + AHEAD, RING)
            start_w(0, k + AHEAD, w_sem.at[nb, 0], w_sem.at[nb, 1])

        @pl.when(k + AHEAD == nch)
        def _():
            start_kv(0)

        @pl.when(k + AHEAD == nch + 1)
        def _():
            start_all_od(0)
        return carry

    with jax.named_scope("kloop"):
        lax.fori_loop(0, nch, l0_body, 0)

    for l in range(layers):
        attention(l)
        with jax.named_scope(f"act{l}"):
            mlp_act()
        if l == 0:
            with jax.named_scope("barrier"):
                pl.semaphore_wait(barrier, tp - 1)
        with jax.named_scope(f"outproj{l}"):
            out_proj(l)
        if l + 1 < layers:
            for k in range(nch):
                start_w(l + 1, k, wl_sem.at[0], wl_sem.at[1])
            start_kv(l + 1)
            start_all_od(l + 1)
        with jax.named_scope(f"reduce{l}"):
            xn = reduce_own(l)
        xg[l + 1, me] = xn
        if l + 1 < layers:
            def use(kind, srcs, l=l):
                if kind == "early":
                    xf = xn.astype(F32)
                    sq = jnp.sum(xf * xf, axis=1, keepdims=True)
                    stats[l, me] = jnp.broadcast_to(sq, (rows, rows)).T[0:8, :]
                    for d in range(1, tp):
                        send(stats.at[l, me], stats.at[l, me], st_s_sem, st_r_sem, lax.rem(me + d, tp))
                    return
                if kind == "own":
                    zero_acc()
                    return
                if kind == "ring" and not use.ready:
                    use.ready = True
                    wait_recv(stats.at[l, 0:tp - 1], st_r_sem)
                    wait_sent(stats.at[l, 0:tp - 1], st_s_sem)
                    arrive(wqkv, wl_sem.at[0])
                    arrive(wgu, wl_sem.at[1])
                    tot = stats[l, 0]
                    for d in range(1, tp):
                        tot = tot + stats[l, d]
                    set_inv_rms(jnp.broadcast_to(tot[0:1, :], (rows, rows)).T[:, 0:1])
                    srcs = [me] + srcs
                for src in srcs:
                    do_chunk(l + 1, src)

            use.ready = False
            with jax.named_scope(f"gather{l}"):
                gather(l, use)
        else:
            def use_out(kind, srcs, l=l):
                for src in srcs:
                    pltpu.make_async_copy(xg.at[l + 1, src], out_hbm.at[:, pl.ds(pl.multiple_of(src * cw, cw), cw)], out_sem).start()

            with jax.named_scope(f"gather{l}"):
                gather(l, use_out)
            with jax.named_scope("outs"):
                arrive(xg.at[l + 1], out_sem)


def solution(mesh):
    tp = mesh.shape["tp"]
    arg_specs = (P("dp", None), P("dp"), P(), P(None, None, "tp"), P(None, None, "tp"), P(None, None, "tp"), P(None, "tp", None),
                 P(None, None, "tp"), P(None, None, "tp"), P(None, "tp", None), P(None, "dp", None, "tp", None), P(None, "dp", None, "tp", None))

    def per_device(x_in, lengths, norm_gain, w_q, w_k, w_v, w_o, w_gate, w_up, w_down, k_cache, v_cache):
        rows, width = x_in.shape
        layers, _, seq, hq, head = k_cache.shape
        ff = w_gate.shape[2]
        cw = width // tp
        chips = tp // 2
        assert w_q.shape[2] == cw == hq * head
        freq = (1.0 / (np.float32(ROPE_BASE) ** (np.arange(0, head, 2).astype(np.float32) / np.float32(head)))).astype(np.float32)
        freq = jnp.asarray(np.concatenate([freq, freq])[None, :])
        ffp = -(-(cw + ff) // 256) * 256 - cw
        kvr = rows * seq * hq
        ngrp = rows // 8
        m = hq * 8
        any_spec = pl.BlockSpec(memory_space=pl.ANY)
        vmem = pl.BlockSpec(memory_space=pltpu.VMEM)
        V = pltpu.VMEM
        D = pltpu.SemaphoreType.DMA
        scratch = [
            V((layers + 1, tp, rows, cw), BF16),
            V((tp, cw, 3 * cw), BF16),
            V((tp, 2, ff, cw), BF16),
            V((chips, cw + ffp, 2 * cw), BF16),
            V((kvr, head), BF16), V((kvr, head), BF16),
            V((layers, width), F32),
            V((rows, cw), F32),
            V((rows, rows), F32),
            V((rows, head), F32), V((rows, head), F32),
            V((rows, 3 * cw), F32),
            V((ff, rows), F32), V((ff, rows), F32),
            V((ffp, rows), F32),
            V((ngrp, hq, 8, head), F32), V((ngrp, hq, 8, head), F32), V((ngrp, hq, 8, head), F32),
            V((rows * hq, 8 * seq * hq), F32),
            V((rows * hq, 8 * seq * hq), BF16),
            V((rows, cw + ffp), BF16),
            V((rows, cw), F32),
            V((layers, chips, rows, cw), F32),
            V((layers, chips, rows, cw), F32),
            V((layers, chips, rows, cw), F32),
            V((layers, chips, rows, cw), BF16),
            V((layers, chips, rows, cw), BF16),
            V((layers, tp, 8, rows), F32),
            D(()), D((RING, 2)), D((2,)), D((2,)), D(()),
            D(()), D((chips,)), D(()), D((chips - 1,)), D(()), D(()),
            D(()), D((2 * NSUB + 5,)), D((chips,)), D(()),
        ]
        cfg = (tp, rows, width, ff, seq, head, hq, layers)
        return pl.pallas_call(
            functools.partial(decode_kernel, cfg),
            out_shape=jax.ShapeDtypeStruct((rows, width), BF16),
            in_specs=[any_spec, vmem, vmem, vmem] + [any_spec] * 9,
            out_specs=any_spec,
            scratch_shapes=scratch,
            compiler_params=pltpu.CompilerParams(collective_id=0, has_side_effects=True, vmem_limit_bytes=60 * 1024 * 1024),
        )(x_in, lengths.reshape(1, rows), freq, norm_gain, w_q, w_k, w_v, w_o, jnp.swapaxes(w_gate, 1, 2), jnp.swapaxes(w_up, 1, 2), w_down,
          k_cache.reshape(layers, kvr, head), v_cache.reshape(layers, kvr, head))

    return jax.shard_map(per_device, mesh=mesh, in_specs=arg_specs, out_specs=P("dp", None), check_vma=False)
```

time: 90.3 us -> 77.5 us (0.86)
  Pallas kernels: 87.9 us -> 75 us
    pallas_call x1, Pallas kernels: 87.9 us -> 75 us  [per_device(): pl.pallas_call(functools.partial(decode_kernel, cfg), out_shape=jax.Shape...]
where the time goes in v2:
time: 77.5 us; the launch traced here: 77.3 us
  Pallas kernels  75 us (97%)
  local copies, waits for them, and re-layouts  2.29 us (3%)
    pallas_call x1, Pallas kernels, per_device(): pl.pallas_call(functools.partial(decode_kernel, cfg), out_shape=jax.Shape...  75 us
    unnamed x1, local copies, waits for them, and re-layouts  2.29 us

profile of v2, /device:TPU:21, one launch (start us, length us, event | category | flops | bytes accessed | tf_op | source)
XLA Modules:
  0.0 77.3 jit_solution(10511641588143354041)
XLA Ops:
  0.0 75.0 %shard_map.127 = bf16[128,4096]{1,0:T(8,128)(2,1)} custom-call(bf16[128,4096]{1,0:T(8,128)(2,1)} %x_hbm.1, s32[1,128]{1,0:T(1,128)} %bitcast.9, f32[1,128]{1,0:T(1,128)} %constant.2.clone.freq_ref, bf16[2,4096]{1,0:T(2,128)(2,1)} %gain_ref.1, bf16[2,4096,256]{2,1,0:T(8,128)(2,1)} %wq_hbm.1, bf16[2,4096,256]{2,1,0:T(8,128)(2,1)} %wk_hbm.1, ...), custom_call_target="tpu_custom_call" | custom-call | tf_op jit(solution)/shard_map/pallas_call | solution.py:429
  75.0 2.3 %copy.15 = bf16[128,4096]{1,0:T(8,128)(2,1)} copy(bf16[128,4096]{1,0:T(8,128)(2,1)} %shard_map.127) | data formatting | bytes 2097152

commit v3 on v2

--- a/solution.py
+++ b/solution.py
@@ -17,17 +17,19 @@
 FIRST = 2
 AHEAD = 7
 RING = 8
-
-
-def decode_kernel(cfg, x_hbm, len_ref, freq_ref, gain_ref, wq_hbm, wk_hbm, wv_hbm, wo_hbm, wg_hbm, wu_hbm, wd_hbm,
-                  kc_hbm, vc_hbm, out_hbm,
-                  xg, wqkv, wgu, wod, kbuf, vbuf, gain_s, rb, lenb, cosb, sinb, acc_qkv, acc_g, acc_u, ut,
+VLIM = 54016
+
+
+def decode_kernel(cfg, x_hbm, len_hbm, freq_hbm, gain_hbm, wq_hbm, wk_hbm, wv_hbm, wo_hbm, wg_hbm, wu_hbm, wd_hbm,
+                  kc_hbm, vc_hbm, out_ref,
+                  len_ref, freq_ref, gain_ref, xg, wqkv, wgu, wod, kbuf, vbuf, gain_s, rb, lenb, cosb, sinb, acc_qkv, acc_g, acc_u, ut,
                   qs, ks, vs, logit_s, prob_s, hbuf, attn_s, own_f, snd_f, rcv_f, shr_snd, shr_rcv, stats,
-                  x_sem, w_sem, wl_sem, kv_sem, od_sem, pair_s_sem, pair_r_sem, rs_s_sem, rs_r_sem, st_s_sem, st_r_sem,
-                  ag_s_sem, ag_r_sem, pf_r_sem, out_sem):
+                  small_sem, x_sem, w_sem, wl_sem, kv_sem, od_sem, pair_s_sem, pair_r_sem, rs_s_sem, rs_r_sem, st_s_sem, st_r_sem,
+                  ag_s_sem, ag_r_sem, pf_r_sem):
     tp, rows, width, ff, seq, head, hq, layers = cfg
     chips = tp // 2
     half = chips // 2
+    pr = rows // NSUB
     cw = width // tp
     me = lax.axis_index("tp")
     z = me // 2
@@ -84,6 +86,10 @@
     def wait_sent(src, sem):
         wait_remote(src, sem).wait_send()
 
+    small = [pltpu.make_async_copy(src, dst, small_sem.at[i])
+             for i, (src, dst) in enumerate(((len_hbm, len_ref), (freq_hbm, freq_ref), (gain_hbm, gain_ref)))]
+    for cp in small:
+        cp.start()
     offs = [half]
     for d in range(half - 1, 0, -1):
         offs += [d, chips - d]
@@ -104,6 +110,8 @@
         for j in range(chips):
             wod[j, cw + ff:, :] = jnp.zeros((pad, 2 * cw), BF16)
         ut[ff:, :] = jnp.zeros((pad, rows), F32)
+    for cp in small:
+        cp.wait()
     gain_s[...] = gain_ref[...].astype(F32)
     lenb[...] = jnp.broadcast_to(len_ref[...].astype(F32), (rows, rows)).T
     ang = lenb[...] * freq_ref[...]
@@ -184,6 +192,10 @@
         for i in range(ut.shape[0] // 128):
             hbuf[:, cw + i * 128:cw + (i + 1) * 128] = ut[i * 128:(i + 1) * 128, :].T.astype(BF16)
 
+    def send_share(l, i, p):
+        r = pl.ds(p * pr, pr)
+        send(shr_snd.at[l, i, r, :], shr_rcv.at[l, i, r, :], rs_s_sem, rs_r_sem.at[p, i], ring_dev(offs[i]))
+
     def out_proj(l):
         arrive(wod.at[:, 0:cw + ff, :], od_sem)
         hv = hbuf[...]
@@ -196,7 +208,7 @@
                 own_f[l, i] = s
             else:
                 shr_snd[l, i] = s.astype(BF16)
-                send(shr_snd.at[l, i], shr_rcv.at[l, i], rs_s_sem, rs_r_sem.at[i], ring_dev(off))
+                send_share(l, i, 0)
 
         for i in range(chips):
             j = lax.rem(z + offs[i], chips)
@@ -209,22 +221,22 @@
                 finish(i - LAG)
         for i in range(chips - LAG, chips):
             finish(i)
+        for p in range(1, NSUB):
+            for i in range(chips - 1):
+                send_share(l, i, p)
         wait_sent(snd_f.at[l], pair_s_sem)
 
-    def reduce_own(l):
-        acc = xg[l, me].astype(F32) + own_f[l, chips - 1]
+    def reduce_own(l, p):
+        r = pl.ds(p * pr, pr)
+        acc = xg[l, me, r, :].astype(F32) + own_f[l, chips - 1, r, :]
         for i in range(chips - 1):
-            wait_recv(shr_rcv.at[l, i], rs_r_sem.at[i])
-            acc = acc + shr_rcv[l, i].astype(F32)
-        wait_sent(shr_snd.at[l, 0:chips - 1], rs_s_sem)
-        return acc.astype(BF16)
-
-    pr = rows // NSUB
+            wait_recv(shr_rcv.at[l, i, r, :], rs_r_sem.at[p, i])
+            acc = acc + shr_rcv[l, i, r, :].astype(F32)
+        xg[l + 1, me, r, :] = acc.astype(BF16)
 
     def gather(l, use):
         dst = l + 1
         flip = 1 - 2 * c
-        first, last = list(range(NSUB)), list(range(NSUB))[::-1]
 
         def piece(src, p):
             return xg.at[dst, src, pl.ds(p * pr, pr), :]
@@ -255,21 +267,25 @@
             wait_recv(whole(src), pf_r_sem.at[slot(d, side)])
             return src
 
-        for i in range(NSUB):
-            ring(piece(me, first[i]), 2, first[i], 2)
-            ring(piece(me, last[i]), 2, last[i], -2)
-        use("early", [])
-        ring(whole(me), 1, 0, 1)
-        ring(whole(me), 1, 0, -1)
-        to_partner(whole(me), 0, 0)
+        for p in range(NSUB):
+            with jax.named_scope(f"reduce{l}p{p}"):
+                reduce_own(l, p)
+            ring(piece(me, p), 2, p, 2)
+            ring(piece(me, p), 2, p, -2)
+            if p == NSUB - 1:
+                use("early", [])
+            ring(piece(me, p), 1, p, 1)
+            ring(piece(me, p), 1, p, -1)
+            to_partner(piece(me, p), 0, 0)
+        wait_sent(shr_snd.at[l, 0:chips - 1], rs_s_sem)
         use("own", [me])
         two = [ring_dev(-2), ring_dev(2)]
-        for i in range(NSUB):
-            for side, p in ((0, first[i]), (1, last[i])):
+        for p in range(NSUB):
+            for side in (0, 1):
                 src = two[side]
                 wait_recv(piece(src, p), sem_of(2, side, p))
                 sg = 1 if side == 0 else -1
-                if i < NSUB // 2:
+                if side == p // (NSUB // 2):
                     ring(piece(src, p), 4, p, 2 * sg)
                 ring(piece(src, p), 3, p, sg)
                 to_partner(piece(src, p), 2, side)
@@ -332,13 +348,10 @@
                 start_w(l + 1, k, wl_sem.at[0], wl_sem.at[1])
             start_kv(l + 1)
             start_all_od(l + 1)
-        with jax.named_scope(f"reduce{l}"):
-            xn = reduce_own(l)
-        xg[l + 1, me] = xn
         if l + 1 < layers:
             def use(kind, srcs, l=l):
                 if kind == "early":
-                    xf = xn.astype(F32)
+                    xf = xg[l + 1, me].astype(F32)
                     sq = jnp.sum(xf * xf, axis=1, keepdims=True)
                     stats[l, me] = jnp.broadcast_to(sq, (rows, rows)).T[0:8, :]
                     for d in range(1, tp):
@@ -367,12 +380,10 @@
         else:
             def use_out(kind, srcs, l=l):
                 for src in srcs:
-                    pltpu.make_async_copy(xg.at[l + 1, src], out_hbm.at[:, pl.ds(pl.multiple_of(src * cw, cw), cw)], out_sem).start()
+                    out_ref[:, pl.ds(pl.multiple_of(src * cw, cw), cw)] = xg[l + 1, src]
 
             with jax.named_scope(f"gather{l}"):
                 gather(l, use_out)
-            with jax.named_scope("outs"):
-                arrive(xg.at[l + 1], out_sem)
 
 
 def solution(mesh):
@@ -393,11 +404,14 @@
         kvr = rows * seq * hq
         ngrp = rows // 8
         m = hq * 8
+        pin = lambda v: pltpu.with_memory_space_constraint(v, pltpu.HBM)
+        hbm = pl.BlockSpec(memory_space=pltpu.HBM)
         any_spec = pl.BlockSpec(memory_space=pl.ANY)
         vmem = pl.BlockSpec(memory_space=pltpu.VMEM)
         V = pltpu.VMEM
         D = pltpu.SemaphoreType.DMA
         scratch = [
+            V((1, rows), jnp.int32), V((1, head), F32), V((layers, width), BF16),
             V((layers + 1, tp, rows, cw), BF16),
             V((tp, cw, 3 * cw), BF16),
             V((tp, 2, ff, cw), BF16),
@@ -421,19 +435,19 @@
             V((layers, chips, rows, cw), BF16),
             V((layers, chips, rows, cw), BF16),
             V((layers, tp, 8, rows), F32),
-            D(()), D((RING, 2)), D((2,)), D((2,)), D(()),
-            D(()), D((chips,)), D(()), D((chips - 1,)), D(()), D(()),
-            D(()), D((2 * NSUB + 5,)), D((chips,)), D(()),
+            D((3,)), D(()), D((RING, 2)), D((2,)), D((2,)), D(()),
+            D(()), D((chips,)), D(()), D((NSUB, chips - 1)), D(()), D(()),
+            D(()), D((2 * NSUB + 5,)), D((chips,)),
         ]
         cfg = (tp, rows, width, ff, seq, head, hq, layers)
         return pl.pallas_call(
             functools.partial(decode_kernel, cfg),
             out_shape=jax.ShapeDtypeStruct((rows, width), BF16),
-            in_specs=[any_spec, vmem, vmem, vmem] + [any_spec] * 9,
-            out_specs=any_spec,
+            in_specs=[any_spec, hbm, hbm, hbm] + [any_spec] * 9,
+            out_specs=vmem,
             scratch_shapes=scratch,
-            compiler_params=pltpu.CompilerParams(collective_id=0, has_side_effects=True, vmem_limit_bytes=60 * 1024 * 1024),
-        )(x_in, lengths.reshape(1, rows), freq, norm_gain, w_q, w_k, w_v, w_o, jnp.swapaxes(w_gate, 1, 2), jnp.swapaxes(w_up, 1, 2), w_down,
+            compiler_params=pltpu.CompilerParams(collective_id=0, has_side_effects=True, vmem_limit_bytes=VLIM * 1024),
+        )(x_in, pin(lengths.reshape(1, rows)), pin(freq), pin(norm_gain), w_q, w_k, w_v, w_o, jnp.swapaxes(w_gate, 1, 2), jnp.swapaxes(w_up, 1, 2), w_down,
           k_cache.reshape(layers, kvr, head), v_cache.reshape(layers, kvr, head))
 
     return jax.shard_map(per_device, mesh=mesh, in_specs=arg_specs, out_specs=P("dp", None), check_vma=False)

time: 77.5 us -> 73.4 us (0.947)
  Pallas kernels: 75 us -> 72.2 us
  local copies, waits for them, and re-layouts: 2.29 us -> 0.97 us
    pallas_call x1, Pallas kernels: 75 us -> 72.2 us  [per_device(): pl.pallas_call(functools.partial(decode_kernel, cfg), out_shape=jax.Shape...]
    unnamed x1, local copies, waits for them, and re-layouts: 2.29 us -> 0.97 us
where the time goes in v3:
time: 73.4 us; the launch traced here: 73.2 us
  Pallas kernels  72.2 us (98%)
  local copies, waits for them, and re-layouts  0.97 us (1%)
    pallas_call x1, Pallas kernels, per_device(): pl.pallas_call(functools.partial(decode_kernel, cfg), out_shape=jax.Shape...  72.2 us

profile of v3, /device:TPU:21, one launch (start us, length us, event | category | flops | bytes accessed | tf_op | source)
XLA Modules:
  0.0 73.2 jit_solution(534091796039206735)
XLA Ops:
  0.0 72.2 %shard_map.127 = bf16[128,4096]{1,0:T(8,128)(2,1)S(1)} custom-call(bf16[128,4096]{1,0:T(8,128)(2,1)} %x_hbm.1, s32[1,128]{1,0:T(1,128)} %bitcast.9, f32[1,128]{1,0:T(1,128)} %constant.2.clone.freq_hbm, bf16[2,4096]{1,0:T(2,128)(2,1)} %gain_hbm.1, bf16[2,4096,256]{2,1,0:T(8,128)(2,1)} %wq_hbm.1, bf16[2,4096,256]{2,1,0:T(8,128)(2,1)} %wk_hbm.1, ...), custom_call_target="tpu_custom_call" | custom-call | tf_op jit(solution)/shard_map/pallas_call | solution.py:443
  72.2 1.0 %copy.15 = bf16[128,4096]{1,0:T(8,128)(2,1)} copy(bf16[128,4096]{1,0:T(8,128)(2,1)S(1)} %shard_map.127) | data formatting | bytes 2097152

commit v4 on v3

--- a/solution.py
+++ b/solution.py
@@ -14,9 +14,12 @@
 BF16 = jnp.bfloat16
 NSUB = 2
 LAG = 3
-FIRST = 2
-AHEAD = 7
+FIRST = 3
+AHEAD = 8
 RING = 8
+UNROLL = 2
+WIDE = 2
+KV_AT = 3
 VLIM = 54016
 
 
@@ -59,14 +62,11 @@
         pltpu.make_async_copy(kc_hbm.at[l], kbuf, kv_sem.at[0]).start()
         pltpu.make_async_copy(vc_hbm.at[l], vbuf, kv_sem.at[1]).start()
 
-    def start_od(l, j):
+    def start_od(l, i):
+        j = lax.rem(z + offs[i], chips)
         cs = pl.ds(j * 2 * cw, 2 * cw)
-        pltpu.make_async_copy(wo_hbm.at[l, :, cs], wod.at[j, 0:cw, :], od_sem).start()
-        pltpu.make_async_copy(wd_hbm.at[l, :, cs], wod.at[j, cw:cw + ff, :], od_sem).start()
-
-    def start_all_od(l):
-        for i in range(chips):
-            start_od(l, lax.rem(z + offs[i], chips))
+        pltpu.make_async_copy(wo_hbm.at[l, :, cs], wod.at[j, 0:cw, :], od_sem.at[i]).start()
+        pltpu.make_async_copy(wd_hbm.at[l, :, cs], wod.at[j, cw:cw + ff, :], od_sem.at[i]).start()
 
     def arrive(ref, sem):
         pltpu.make_async_copy(ref, ref, sem).wait()
@@ -112,6 +112,8 @@
         ut[ff:, :] = jnp.zeros((pad, rows), F32)
     for cp in small:
         cp.wait()
+    for k in range(FIRST, AHEAD):
+        start_w(0, k, w_sem.at[k, 0], w_sem.at[k, 1])
     gain_s[...] = gain_ref[...].astype(F32)
     lenb[...] = jnp.broadcast_to(len_ref[...].astype(F32), (rows, rows)).T
     ang = lenb[...] * freq_ref[...]
@@ -125,14 +127,20 @@
         inv = lax.rsqrt(ssq / width + NORM_EPS)
         rb[...] = jnp.broadcast_to(inv, rb.shape)
 
-    def do_chunk(l, k):
-        xk = xg[l, k].astype(F32)
-        g = gain_s[l:l + 1, pl.ds(pl.multiple_of(k * cw, cw), cw)]
-        a = (xk * rb[...] * g).astype(BF16)
-        acc_qkv[...] += jnp.dot(a, wqkv[k], preferred_element_type=F32)
+    def do_chunks(l, ks):
         nt = (((1,), (1,)), ((), ()))
-        acc_g[...] += lax.dot_general(wgu[k, 0], a, nt, preferred_element_type=F32)
-        acc_u[...] += lax.dot_general(wgu[k, 1], a, nt, preferred_element_type=F32)
+
+        def join(parts, axis):
+            return parts[0] if len(parts) == 1 else jnp.concatenate(parts, axis=axis)
+
+        a = []
+        for k in ks:
+            g = gain_s[l:l + 1, pl.ds(pl.multiple_of(k * cw, cw), cw)]
+            a.append((xg[l, k].astype(F32) * rb[...] * g).astype(BF16))
+        a = join(a, 1)
+        acc_qkv[...] += jnp.dot(a, join([wqkv[k] for k in ks], 0), preferred_element_type=F32)
+        acc_g[...] += lax.dot_general(join([wgu[k, 0] for k in ks], 1), a, nt, preferred_element_type=F32)
+        acc_u[...] += lax.dot_general(join([wgu[k, 1] for k in ks], 1), a, nt, preferred_element_type=F32)
 
     def rope(v):
         return (v * cosb[...] + pltpu.roll(v, head // 2, 1) * sinb[...]).astype(BF16).astype(F32)
@@ -197,7 +205,6 @@
         send(shr_snd.at[l, i, r, :], shr_rcv.at[l, i, r, :], rs_s_sem, rs_r_sem.at[p, i], ring_dev(offs[i]))
 
     def out_proj(l):
-        arrive(wod.at[:, 0:cw + ff, :], od_sem)
         hv = hbuf[...]
 
         def finish(i):
@@ -212,6 +219,7 @@
 
         for i in range(chips):
             j = lax.rem(z + offs[i], chips)
+            arrive(wod.at[j, 0:cw + ff, :], od_sem.at[i])
             p = jnp.dot(hv, wod[j], preferred_element_type=F32)
             lo, hi = p[:, :cw], p[:, cw:]
             own_f[l, i] = jnp.where(c == 0, lo, hi)
@@ -303,36 +311,37 @@
     with jax.named_scope("stats"):
         ssq = jnp.zeros((rows, cw), F32)
         arrive(xg.at[0], x_sem)
-        for k in range(FIRST, AHEAD):
-            start_w(0, k, w_sem.at[k, 0], w_sem.at[k, 1])
         for k in range(nch):
             xf = xg[0, k].astype(F32)
             ssq = ssq + xf * xf
         set_inv_rms(jnp.sum(ssq, axis=1, keepdims=True))
         zero_acc()
 
-    def l0_body(k, carry):
-        b = lax.rem(k, RING)
-        arrive(wqkv.at[k], w_sem.at[b, 0])
-        arrive(wgu.at[k], w_sem.at[b, 1])
-        do_chunk(0, k)
-
-        @pl.when(k + AHEAD < nch)
-        def _():
-            nb = lax.rem(k + AHEAD, RING)
-            start_w(0, k + AHEAD, w_sem.at[nb, 0], w_sem.at[nb, 1])
-
-        @pl.when(k + AHEAD == nch)
+    def l0_body(i, carry):
+        ks = [i * UNROLL + u for u in range(UNROLL)]
+        for k in ks:
+            b = lax.rem(k, RING)
+            arrive(wqkv.at[k], w_sem.at[b, 0])
+            arrive(wgu.at[k], w_sem.at[b, 1])
+        for k in ks:
+            @pl.when(k + AHEAD < nch)
+            def _(k=k):
+                nb = lax.rem(k + AHEAD, RING)
+                start_w(0, k + AHEAD, w_sem.at[nb, 0], w_sem.at[nb, 1])
+
+        @pl.when(i == KV_AT)
         def _():
             start_kv(0)
-
-        @pl.when(k + AHEAD == nch + 1)
-        def _():
-            start_all_od(0)
+        for b in range(chips // 2):
+            @pl.when(i == (nch - AHEAD) // UNROLL + b)
+            def _(b=b):
+                start_od(0, 2 * b)
+                start_od(0, 2 * b + 1)
+        do_chunks(0, ks)
         return carry
 
     with jax.named_scope("kloop"):
-        lax.fori_loop(0, nch, l0_body, 0)
+        lax.fori_loop(0, nch // UNROLL, l0_body, 0)
 
     for l in range(layers):
         attention(l)
@@ -347,13 +356,14 @@
             for k in range(nch):
                 start_w(l + 1, k, wl_sem.at[0], wl_sem.at[1])
             start_kv(l + 1)
-            start_all_od(l + 1)
+            for i in range(chips):
+                start_od(l + 1, i)
         if l + 1 < layers:
             def use(kind, srcs, l=l):
                 if kind == "early":
                     xf = xg[l + 1, me].astype(F32)
                     sq = jnp.sum(xf * xf, axis=1, keepdims=True)
-                    stats[l, me] = jnp.broadcast_to(sq, (rows, rows)).T[0:8, :]
+                    stats[l, me] = jnp.broadcast_to(sq, (rows, rows)).T[0:1, :]
                     for d in range(1, tp):
                         send(stats.at[l, me], stats.at[l, me], st_s_sem, st_r_sem, lax.rem(me + d, tp))
                     return
@@ -369,10 +379,10 @@
                     tot = stats[l, 0]
                     for d in range(1, tp):
                         tot = tot + stats[l, d]
-                    set_inv_rms(jnp.broadcast_to(tot[0:1, :], (rows, rows)).T[:, 0:1])
+                    set_inv_rms(jnp.broadcast_to(tot, (rows, rows)).T[:, 0:1])
                     srcs = [me] + srcs
-                for src in srcs:
-                    do_chunk(l + 1, src)
+                for n in range(0, len(srcs), WIDE):
+                    do_chunks(l + 1, srcs[n:n + WIDE])
 
             use.ready = False
             with jax.named_scope(f"gather{l}"):
@@ -434,8 +444,8 @@
             V((layers, chips, rows, cw), F32),
             V((layers, chips, rows, cw), BF16),
             V((layers, chips, rows, cw), BF16),
-            V((layers, tp, 8, rows), F32),
-            D((3,)), D(()), D((RING, 2)), D((2,)), D((2,)), D(()),
+            V((layers, tp, 1, rows), F32),
+            D((3,)), D(()), D((RING, 2)), D((2,)), D((2,)), D((chips,)),
             D(()), D((chips,)), D(()), D((NSUB, chips - 1)), D(()), D(()),
             D(()), D((2 * NSUB + 5,)), D((chips,)),
         ]

time: 73.4 us -> 71.3 us (0.971)
  Pallas kernels: 72.2 us -> 70.3 us
    pallas_call x1, Pallas kernels: 72.2 us -> 70.3 us  [per_device(): pl.pallas_call(functools.partial(decode_kernel, cfg), out_shape=jax.Shape...]
where the time goes in v4:
time: 71.3 us; the launch traced here: 71.2 us
  Pallas kernels  70.3 us (99%)
  local copies, waits for them, and re-layouts  0.97 us (1%)
    pallas_call x1, Pallas kernels, per_device(): pl.pallas_call(functools.partial(decode_kernel, cfg), out_shape=jax.Shape...  70.3 us

profile of v4, /device:TPU:21, one launch (start us, length us, event | category | flops | bytes accessed | tf_op | source)
XLA Modules:
  0.0 71.2 jit_solution(12632402114985422377)
XLA Ops:
  0.0 70.3 %shard_map.127 = bf16[128,4096]{1,0:T(8,128)(2,1)S(1)} custom-call(bf16[128,4096]{1,0:T(8,128)(2,1)} %x_hbm.1, s32[1,128]{1,0:T(1,128)} %bitcast.9, f32[1,128]{1,0:T(1,128)} %constant.2.clone.freq_hbm, bf16[2,4096]{1,0:T(2,128)(2,1)} %gain_hbm.1, bf16[2,4096,256]{2,1,0:T(8,128)(2,1)} %wq_hbm.1, bf16[2,4096,256]{2,1,0:T(8,128)(2,1)} %wk_hbm.1, ...), custom_call_target="tpu_custom_call" | custom-call | tf_op jit(solution)/shard_map/pallas_call | solution.py:453
  70.3 1.0 %copy.15 = bf16[128,4096]{1,0:T(8,128)(2,1)} copy(bf16[128,4096]{1,0:T(8,128)(2,1)S(1)} %shard_map.127) | data formatting | bytes 2097152

commit v5 on v4

--- a/solution.py
+++ b/solution.py
@@ -116,11 +116,6 @@
         start_w(0, k, w_sem.at[k, 0], w_sem.at[k, 1])
     gain_s[...] = gain_ref[...].astype(F32)
     lenb[...] = jnp.broadcast_to(len_ref[...].astype(F32), (rows, rows)).T
-    ang = lenb[...] * freq_ref[...]
-    lane = lax.broadcasted_iota(jnp.int32, (rows, head), 1)
-    cosb[...] = jnp.cos(ang)
-    sn = jnp.sin(ang)
-    sinb[...] = jnp.where(lane < head // 2, -sn, sn)
     scope_pre.__exit__(None, None, None)
 
     def set_inv_rms(ssq):
@@ -304,8 +299,8 @@
         far = [arrived(4, 0)]
         use("pair", [from_partner(1, 0), from_partner(1, 1)])
         use("ring", three + far)
-        for d, side in ((3, 0), (3, 1), (4, 0)):
-            use("pair", [from_partner(d, side)])
+        use("pair", [from_partner(3, 0), from_partner(3, 1)])
+        use("pair", [from_partner(4, 0)])
         wait_sent(xg.at[dst, 0:7 + 2 * half], ag_s_sem)
 
     with jax.named_scope("stats"):
@@ -316,6 +311,8 @@
             ssq = ssq + xf * xf
         set_inv_rms(jnp.sum(ssq, axis=1, keepdims=True))
         zero_acc()
+
+    rope_rows = rows * UNROLL // nch
 
     def l0_body(i, carry):
         ks = [i * UNROLL + u for u in range(UNROLL)]
@@ -332,16 +329,23 @@
         @pl.when(i == KV_AT)
         def _():
             start_kv(0)
-        for b in range(chips // 2):
-            @pl.when(i == (nch - AHEAD) // UNROLL + b)
+        for b in range(2):
+            @pl.when(i == nch // UNROLL - 2 + b)
             def _(b=b):
                 start_od(0, 2 * b)
                 start_od(0, 2 * b + 1)
+        r = pl.ds(pl.multiple_of(i * rope_rows, rope_rows), rope_rows)
+        ang = lenb[r, :] * freq_ref[...]
+        sn = jnp.sin(ang)
+        cosb[r, :] = jnp.cos(ang)
+        sinb[r, :] = jnp.where(lax.broadcasted_iota(jnp.int32, sn.shape, 1) < head // 2, -sn, sn)
         do_chunks(0, ks)
         return carry
 
     with jax.named_scope("kloop"):
         lax.fori_loop(0, nch // UNROLL, l0_body, 0)
+        for b in range(4, chips):
+            start_od(0, b)
 
     for l in range(layers):
         attention(l)

time: 71.3 us -> 71.5 us (level)
  no operation moved by 1% of the time
where the time goes in v5:
time: 71.5 us; the launch traced here: 71.4 us
  Pallas kernels  70.4 us (98%)
  local copies, waits for them, and re-layouts  0.97 us (1%)
    pallas_call x1, Pallas kernels, per_device(): pl.pallas_call(functools.partial(decode_kernel, cfg), out_shape=jax.Shape...  70.4 us

profile of v5, /device:TPU:21, one launch (start us, length us, event | category | flops | bytes accessed | tf_op | source)
XLA Modules:
  0.0 71.4 jit_solution(287983651170147725)
XLA Ops:
  0.0 70.4 %shard_map.127 = bf16[128,4096]{1,0:T(8,128)(2,1)S(1)} custom-call(bf16[128,4096]{1,0:T(8,128)(2,1)} %x_hbm.1, s32[1,128]{1,0:T(1,128)} %bitcast.9, f32[1,128]{1,0:T(1,128)} %constant.2.clone.freq_hbm, bf16[2,4096]{1,0:T(2,128)(2,1)} %gain_hbm.1, bf16[2,4096,256]{2,1,0:T(8,128)(2,1)} %wq_hbm.1, bf16[2,4096,256]{2,1,0:T(8,128)(2,1)} %wk_hbm.1, ...), custom_call_target="tpu_custom_call" | custom-call | tf_op jit(solution)/shard_map/pallas_call | solution.py:457
  70.4 1.0 %copy.15 = bf16[128,4096]{1,0:T(8,128)(2,1)} copy(bf16[128,4096]{1,0:T(8,128)(2,1)S(1)} %shard_map.127) | data formatting | bytes 2097152
